TPU v7x, 32 devices: a whole 2x2x4 slice. The times are simulated.
32 devices in a mesh: row: 16 (over z, y, core), col: 2 (over x).
Axes of the slice: x: 2, y: 2, z: 4, core: 2. Of those that a mesh axis runs over, the one named last changes fastest.
Arguments:
- spectral_field: float32 [2, 256, 256, 256], P(None, 'row', 'col'), may hold values from -4.5 to 4.5
Outputs:
- updated_field: float32 [2, 256, 256, 256], P(None, 'row', 'col')
- shell_spectrum: float32 [256], replicated
All inputs are finite; a program needn't handle non-finite values.
Results may differ from a plain program's by a relative error of at most 0.0031.
Values may be sent and summed in bfloat16 or wider, within the bound.
A program may use at most 192 MiB of HBM per device.

v0:
```python
import math

import jax
import jax.numpy as jnp
from jax import lax
from jax.sharding import PartitionSpec as P

phase_rate = 0.0002
coupling = 0.2


def wave_table(inputs, outputs, length, sine_sign, live_mask):
    phase_turns = jnp.mod(inputs[:, None] * outputs[None, :], length)
    phase_angle = phase_turns.astype(jnp.float32) * (2.0 * math.pi / length)
    live_rows = live_mask.astype(jnp.float32)[:, None]
    cosine_part = (jnp.cos(phase_angle) * live_rows).astype(jnp.bfloat16)
    sine_part = (sine_sign * jnp.sin(phase_angle) * live_rows).astype(jnp.bfloat16)
    return (cosine_part, sine_part)


def rotate(values_in, cosine_part, sine_part, einsum_form, factor):

    def product(first_arg, second_arg):
        return jnp.einsum(einsum_form, first_arg, second_arg, preferred_element_type=jnp.float32)

    out_real = product(values_in[0], cosine_part) - product(values_in[1], sine_part)
    out_imag = product(values_in[0], sine_part) + product(values_in[1], cosine_part)
    return jnp.stack([out_real, out_imag]) * factor


def layout(block_size, owners, stretch, mode_count):
    position = jnp.arange(block_size * owners * stretch, dtype=jnp.int32)
    owner_index = position // (block_size * stretch)
    offset = position % (block_size * stretch)
    is_real = offset < block_size
    kept_wave = owner_index * block_size + offset - mode_count // 2
    extra_wave = mode_count // 2 + owner_index * block_size + offset - block_size
    return (jnp.where(is_real, kept_wave, extra_wave), is_real)


def body(spectral_field):
    width_x = spectral_field.shape[1]
    width_y = spectral_field.shape[2]
    mode_count = spectral_field.shape[3]
    row_count = lax.axis_size("row")
    col_count = lax.axis_size("col")
    grid_count = 2 * mode_count
    half_modes = mode_count // 2
    scale_in = 1.0 / math.sqrt(mode_count)
    scale_out = math.sqrt(mode_count) / grid_count
    stretch = 1
    grid_points = jnp.arange(grid_count, dtype=jnp.int32)
    every_point = jnp.ones((grid_count,), bool)
    wave_x, real_x = layout(width_x, row_count, stretch, mode_count)
    wave_y, real_y = layout(width_y, col_count, stretch, mode_count)
    wave_z, real_z = layout(mode_count, 1, stretch, mode_count)
    inv_x = wave_table(wave_x, grid_points, grid_count, 1.0, real_x)
    inv_y = wave_table(wave_y, grid_points, grid_count, 1.0, real_y)
    inv_z = wave_table(wave_z, grid_points, grid_count, 1.0, real_z)
    fwd_x = wave_table(grid_points, wave_x, grid_count, -1.0, every_point)
    fwd_y = wave_table(grid_points, wave_y, grid_count, -1.0, every_point)
    fwd_z = wave_table(grid_points, wave_z, grid_count, -1.0, every_point)
    coeffs = spectral_field.astype(jnp.bfloat16)
    along_z = rotate(coeffs, inv_z[0], inv_z[1], "abc,cd->abd", scale_in).astype(jnp.bfloat16)
    along_y = rotate(
        lax.all_to_all(along_z, "col", split_axis=3, concat_axis=2, tiled=True),
        inv_y[0],
        inv_y[1],
        "abc,bd->acd",
        scale_in,
    ).astype(jnp.bfloat16)
    physical = rotate(
        lax.all_to_all(along_y, "row", split_axis=3, concat_axis=1, tiled=True),
        inv_x[0],
        inv_x[1],
        "abc,ad->bcd",
        scale_in,
    )
    cubic_term = (
        coupling * (physical[0] * physical[0] + physical[1] * physical[1]) * physical
    ).astype(jnp.bfloat16)
    back_x = rotate(cubic_term, fwd_x[0], fwd_x[1], "abc,cd->abd", scale_out).astype(jnp.bfloat16)
    back_y = rotate(
        lax.all_to_all(back_x, "row", split_axis=3, concat_axis=2, tiled=True),
        fwd_y[0],
        fwd_y[1],
        "abc,bd->acd",
        scale_out,
    ).astype(jnp.bfloat16)
    nonlinear = rotate(
        lax.all_to_all(back_y, "col", split_axis=3, concat_axis=1, tiled=True),
        fwd_z[0],
        fwd_z[1],
        "abc,ad->bcd",
        scale_out,
    )
    local_x = lax.axis_index("row") * width_x + jnp.arange(width_x, dtype=jnp.int32) - half_modes
    local_y = lax.axis_index("col") * width_y + jnp.arange(width_y, dtype=jnp.int32) - half_modes
    local_z = jnp.arange(mode_count, dtype=jnp.int32) - half_modes
    squared = (
        local_x[:, None, None] * local_x[:, None, None]
        + local_y[None, :, None] * local_y[None, :, None]
        + local_z[None, None, :] * local_z[None, None, :]
    )
    phase_angle = phase_rate * squared.astype(jnp.float32)
    cosine_part = jnp.cos(phase_angle)
    sine_part = jnp.sin(phase_angle)
    shifted_real = spectral_field[0] - nonlinear[1]
    shifted_imag = spectral_field[1] + nonlinear[0]
    new_real = shifted_real * cosine_part + shifted_imag * sine_part
    new_imag = shifted_imag * cosine_part - shifted_real * sine_part
    updated_field = jnp.stack([new_real, new_imag])
    energy = new_real * new_real + new_imag * new_imag
    shell_index = jnp.floor(jnp.sqrt(squared.astype(jnp.float32)) + 0.5).astype(jnp.int32)
    shell_bins = jnp.arange(mode_count, dtype=jnp.int32)

    def per_plane(plane_pair):
        plane_energy, plane_shell = plane_pair
        one_hot = (plane_shell.reshape(-1)[:, None] == shell_bins[None, :]).astype(jnp.float32)
        plane_total = jnp.dot(plane_energy.reshape(-1), one_hot, precision=lax.Precision.HIGHEST)
        return (plane_total, jnp.sum(one_hot, axis=0))

    plane_totals, plane_counts = lax.map(per_plane, (energy, shell_index))
    totals, counts = lax.psum(
        (jnp.sum(plane_totals, axis=0), jnp.sum(plane_counts, axis=0)), ("row", "col")
    )
    shell_spectrum = totals / jnp.maximum(counts, 1.0)
    return (updated_field, shell_spectrum)


def solution(mesh):
    in_specs = (P(None, "row", "col", None),)
    out_specs = (P(None, "row", "col", None), P())
    return jax.shard_map(body, mesh=mesh, in_specs=in_specs, out_specs=out_specs, check_vma=False)
```

profile of v0, /device:TPU:0, one launch (start us, length us, event | category | flops | bytes accessed | tf_op | source)
XLA Modules:
  0.0 1367.9 jit_solution(1420235218202868640)
XLA Ops:
  25.3 48.8 %all-to-all-done = bf16[2,16,128,512]{2,1,0,3:T(8,128)(2,1)} async-done(((bf16[2,16,128,512]{2,1,0,3:T(8,128)(2,1)}), bf16[2,16,128,512]{2,1,0,3:T(8,128)(2,1)}, u32[]{:S(2)}, u32[]{:S(2)}) %all-to-all-start) | async-done | bytes 4194336 | tf_op jit(solution)/shard_map/all_to_all | solution.py:66
  116.6 14.6 %copy.67 = bf16[2,16,256,512]{2,1,0,3:T(8,128)(2,1)} copy(bf16[2,16,256,512]{3,2,1,0:T(8,128)(2,1)} %fusion.10) | data formatting | bytes 16777216 | tf_op jit(solution)/shard_map/convert_element_type | solution.py:71
  137.8 150.5 %all-to-all-done.1 = bf16[2,16,256,512]{2,1,0,3:T(8,128)(2,1)} async-done(((bf16[2,16,256,512]{2,1,0,3:T(8,128)(2,1)}), bf16[2,16,256,512]{2,1,0,3:T(8,128)(2,1)}, u32[]{:S(2)}, u32[]{:S(2)}) %all-to-all-start.1) | async-done | bytes 8388640 | tf_op jit(solution)/shard_map/all_to_all | solution.py:73
  354.0 18.7 %add_bitcast_fusion = f32[1,256,32,512]{3,1,2,0:T(8,128)} fusion(f32[256,32,512]{2,0,1:T(8,128)} %fusion.91, bf16[256,256,32]{0,1,2:T(8,128)(2,1)} %copy.72, f32[256]{0:T(256)S(1)} %fusion.115, s32[256]{0:T(256)S(1)} %add_select_fusion.6), kind=kOutput, calls=%fused_computation.20 | convolution fusion | flops 2153775104 | bytes 37750784 | tf_op jit(solution)/shard_map/abc,ad->bcd/dot_general | solution.py:24
  372.8 19.0 %fusion.6 = f32[2,256,32,512]{3,1,2,0:T(8,128)} fusion(f32[1,256,32,512]{3,1,2,0:T(8,128)} %add_bitcast_fusion, f32[1,256,32,512]{3,1,2,0:T(8,128)S(1)} %subtract_bitcast_fusion), kind=kLoop, calls=%fused_computation.10 | loop fusion | flops 16777216 | bytes 67108864 | tf_op jit(solution)/shard_map/mul | solution.py:28
  391.7 17.3 %fusion.9 = f32[256,32,512]{2,0,1:T(8,128)} fusion(f32[2,256,32,512]{3,1,2,0:T(8,128)} %fusion.6), kind=kLoop, calls=%fused_computation.14 | loop fusion | flops 16777216 | bytes 50331648 | tf_op jit(solution)/shard_map/mul | solution.py:80
  409.1 23.1 %multiply_convert_fusion = bf16[2,256,32,512]{3,1,2,0:T(8,128)(2,1)} fusion(f32[1,256,32,512]{3,1,2,0:T(8,128)} %add_bitcast_fusion, f32[1,256,32,512]{3,1,2,0:T(8,128)} %copy-done, f32[256,32,512]{2,0,1:T(8,128)} %fusion.9), kind=kLoop, calls=%fused_computation.9 | loop fusion | flops 25165824 | bytes 67108864 | tf_op jit(solution)/shard_map/convert_element_type | solution.py:81
  482.4 14.6 %copy.75 = bf16[2,256,32,256]{1,2,0,3:T(8,128)(2,1)} copy(bf16[2,256,32,256]{3,1,2,0:T(8,128)(2,1)} %fusion.11) | data formatting | bytes 16777216 | tf_op jit(solution)/shard_map/convert_element_type | solution.py:82
  497.1 218.6 %all_to_all.60 = bf16[2,256,32,256]{1,2,0,3:T(8,128)(2,1)} all-to-all(bf16[2,256,32,256]{1,2,0,3:T(8,128)(2,1)} %copy.75), channel_id=1, replica_groups=mesh['row'=16,'col'=2] {'row'}, dimensions={3} | all-to-all | bytes 16777216 | tf_op jit(solution)/shard_map/all_to_all | solution.py:84
  793.6 48.7 %all-to-all-done.3 = bf16[2,256,16,256]{1,2,0,3:T(8,128)(2,1)} async-done(((bf16[2,256,16,256]{1,2,0,3:T(8,128)(2,1)}), bf16[2,256,16,256]{1,2,0,3:T(8,128)(2,1)}, u32[]{:S(2)}, u32[]{:S(2)}) %all-to-all-start.3) | async-done | bytes 4194336 | tf_op jit(solution)/shard_map/all_to_all | solution.py:91
  899.0 424.4 %while.13 = (s32[]{:T(128)}, f32[16,256]{1,0:T(8,128)S(1)}, f32[16,256]{1,0:T(8,128)S(1)}, f32[16,128,256]{2,1,0:T(8,128)}, s32[16,128,256]{2,1,0:T(8,128)}, /*index=5*/s32[]{:T(128)}, s32[]{:T(128)}) while((s32[]{:T(128)}, f32[16,256]{1,0:T(8,128)S(1)}, f32[16,256]{1,0:T(8,128)S(1)}, f32[16,128,256]{2,1,0:T(8,128)}, ...), condition=%wide.region_2.3_spmd.clone, body=%wide.region_0.2_spmd.clone.sunk | while | flops 134217472 | bytes 1448029 | solution.py:123
  911.4 14.3 %fusion.246 = f32[256]{0:T(256)S(1)} fusion(s32[32768]{0:T(1024)S(1)} %bitcast.195), kind=kLoop, calls=%fused_computation.4.clone.1 | loop fusion | flops 25165568 | bytes 132096 | tf_op jit(solution)/shard_map/while/body/eval_jaxpr/reduce_sum | solution.py:121
  937.9 14.3 %fusion.246 = f32[256]{0:T(256)S(1)} fusion(s32[32768]{0:T(1024)S(1)} %bitcast.195), kind=kLoop, calls=%fused_computation.4.clone.1 | loop fusion | flops 25165568 | bytes 132096 | tf_op jit(solution)/shard_map/while/body/eval_jaxpr/reduce_sum | solution.py:121
  964.4 14.3 %fusion.246 = f32[256]{0:T(256)S(1)} fusion(s32[32768]{0:T(1024)S(1)} %bitcast.195), kind=kLoop, calls=%fused_computation.4.clone.1 | loop fusion | flops 25165568 | bytes 132096 | tf_op jit(solution)/shard_map/while/body/eval_jaxpr/reduce_sum | solution.py:121
  990.9 14.3 %fusion.246 = f32[256]{0:T(256)S(1)} fusion(s32[32768]{0:T(1024)S(1)} %bitcast.195), kind=kLoop, calls=%fused_computation.4.clone.1 | loop fusion | flops 25165568 | bytes 132096 | tf_op jit(solution)/shard_map/while/body/eval_jaxpr/reduce_sum | solution.py:121
  1017.4 14.3 %fusion.246 = f32[256]{0:T(256)S(1)} fusion(s32[32768]{0:T(1024)S(1)} %bitcast.195), kind=kLoop, calls=%fused_computation.4.clone.1 | loop fusion | flops 25165568 | bytes 132096 | tf_op jit(solution)/shard_map/while/body/eval_jaxpr/reduce_sum | solution.py:121
  1043.9 14.3 %fusion.246 = f32[256]{0:T(256)S(1)} fusion(s32[32768]{0:T(1024)S(1)} %bitcast.195), kind=kLoop, calls=%fused_computation.4.clone.1 | loop fusion | flops 25165568 | bytes 132096 | tf_op jit(solution)/shard_map/while/body/eval_jaxpr/reduce_sum | solution.py:121
  1097.0 14.3 %fusion.246 = f32[256]{0:T(256)S(1)} fusion(s32[32768]{0:T(1024)S(1)} %bitcast.195), kind=kLoop, calls=%fused_computation.4.clone.1 | loop fusion | flops 25165568 | bytes 132096 | tf_op jit(solution)/shard_map/while/body/eval_jaxpr/reduce_sum | solution.py:121
  1123.5 14.3 %fusion.246 = f32[256]{0:T(256)S(1)} fusion(s32[32768]{0:T(1024)S(1)} %bitcast.195), kind=kLoop, calls=%fused_computation.4.clone.1 | loop fusion | flops 25165568 | bytes 132096 | tf_op jit(solution)/shard_map/while/body/eval_jaxpr/reduce_sum | solution.py:121
  1150.0 14.3 %fusion.246 = f32[256]{0:T(256)S(1)} fusion(s32[32768]{0:T(1024)S(1)} %bitcast.195), kind=kLoop, calls=%fused_computation.4.clone.1 | loop fusion | flops 25165568 | bytes 132096 | tf_op jit(solution)/shard_map/while/body/eval_jaxpr/reduce_sum | solution.py:121
  1176.5 14.3 %fusion.246 = f32[256]{0:T(256)S(1)} fusion(s32[32768]{0:T(1024)S(1)} %bitcast.195), kind=kLoop, calls=%fused_computation.4.clone.1 | loop fusion | flops 25165568 | bytes 132096 | tf_op jit(solution)/shard_map/while/body/eval_jaxpr/reduce_sum | solution.py:121
  1203.0 14.3 %fusion.246 = f32[256]{0:T(256)S(1)} fusion(s32[32768]{0:T(1024)S(1)} %bitcast.195), kind=kLoop, calls=%fused_computation.4.clone.1 | loop fusion | flops 25165568 | bytes 132096 | tf_op jit(solution)/shard_map/while/body/eval_jaxpr/reduce_sum | solution.py:121
  1229.5 14.3 %fusion.246 = f32[256]{0:T(256)S(1)} fusion(s32[32768]{0:T(1024)S(1)} %bitcast.195), kind=kLoop, calls=%fused_computation.4.clone.1 | loop fusion | flops 25165568 | bytes 132096 | tf_op jit(solution)/shard_map/while/body/eval_jaxpr/reduce_sum | solution.py:121
  1323.5 39.4 %all-reduce = (f32[256]{0:T(256)S(1)}, f32[256]{0:T(256)S(1)}) all-reduce(f32[256]{0:T(256)S(1)} %reduce_sum.27, f32[256]{0:T(256)S(1)} %reduce_sum.28), channel_id=1, replica_groups=mesh['row'=16,'col'=2] {'row','col'}, use_global_device_ids=true, to_apply=%region_4.5 | all-reduce | flops 512 | bytes 4096 | tf_op jit(solution)/shard_map/psum | solution.py:124
  (220 shorter events, 580.3 us)
Async XLA Ops:
  0.6 10.4 copy-start.14
  19.6 54.5 %all-to-all-start = ((bf16[2,16,128,512]{2,1,0,3:T(8,128)(2,1)}), bf16[2,16,128,512]{2,1,0,3:T(8,128)(2,1)}, u32[]{:S(2)}, u32[]{:S(2)}) async-start(bf16[2,16,128,512]{2,1,0,3:T(8,128)(2,1)} %copy.65), calls=%async_computation | async-start | bytes 8388608 | tf_op jit(solution)/shard_map/all_to_all | solution.py:66
  25.2 83.3 %copy-start.12 = (s32[256]{0:T(256)}, s32[256]{0:T(256)S(1)}, u32[]{:S(2)}) copy-start(s32[256]{0:T(256)S(1)} %add_select_fusion.7) | copy-start | bytes 3076
  102.3 6.3 copy-start.6
  131.1 157.2 %all-to-all-start.1 = ((bf16[2,16,256,512]{2,1,0,3:T(8,128)(2,1)}), bf16[2,16,256,512]{2,1,0,3:T(8,128)(2,1)}, u32[]{:S(2)}, u32[]{:S(2)}) async-start(bf16[2,16,256,512]{2,1,0,3:T(8,128)(2,1)} %copy.67), calls=%async_computation.1 | async-start | bytes 16777216 | tf_op jit(solution)/shard_map/all_to_all | solution.py:73
  315.0 10.5 copy-start.1
  325.5 8.1 copy-start.8
  354.0 18.8 %copy-start = (f32[1,256,32,512]{3,1,2,0:T(8,128)}, f32[1,256,32,512]{3,1,2,0:T(8,128)S(1)}, u32[]{:S(2)}) copy-start(f32[1,256,32,512]{3,1,2,0:T(8,128)S(1)} %subtract_bitcast_fusion) | copy-start | bytes 50331652
  432.2 11.0 copy-start.2
  734.7 7.5 copy-start.13
  742.3 8.1 copy-start.4
  750.4 5.8 copy-start.9
  766.2 7.9 copy-start.3
  766.2 7.9 copy-start.7
  787.9 54.4 %all-to-all-start.3 = ((bf16[2,256,16,256]{1,2,0,3:T(8,128)(2,1)}), bf16[2,256,16,256]{1,2,0,3:T(8,128)(2,1)}, u32[]{:S(2)}, u32[]{:S(2)}) async-start(bf16[2,256,16,256]{1,2,0,3:T(8,128)(2,1)} %copy.83), calls=%async_computation.3 | async-start | bytes 8388608 | tf_op jit(solution)/shard_map/all_to_all | solution.py:91
  852.8 2.6 copy-start.15
  855.4 6.0 copy-start.11
  868.9 4.7 copy-start.10
  876.3 2.2 copy-start.5
where the time goes:
time: 1380 us; the launch traced here: 1370 us
  other arithmetic  335 us (24%)
  matrix products  323 us (23%)
  blocking collectives  258 us (19%)
  waiting for transfers between devices  248 us (18%)
  local copies, waits for them, and re-layouts  184 us (13%)
  starting transfers between devices  17.9 us (1%)
    reduce_sum x16, other arithmetic, per_plane(): return (plane_total, jnp.sum(one_hot, axis=0))  229 us
    all_to_all x1, blocking collectives, body(): lax.all_to_all(back_x, 'row', split_axis=3, concat_axis=2, tiled=True)  219 us
    dot_general x24, matrix products, product(): jnp.einsum(einsum_form, first_arg, second_arg, preferred_element_type=jnp...  162 us
    dot_general x16, matrix products, per_plane(): jnp.dot(plane_energy.reshape(-1), one_hot, precision=lax.Precision.HIGHEST)  161 us
    all_to_all x1, waiting for transfers between devices, body(): lax.all_to_all(along_y, 'row', split_axis=3, concat_axis=1, tiled=True)  151 us
    all_to_all x1, waiting for transfers between devices, body(): lax.all_to_all(along_z, 'col', split_axis=3, concat_axis=2, tiled=True)  48.8 us
    all_to_all x1, waiting for transfers between devices, body(): lax.all_to_all(back_y, 'col', split_axis=3, concat_axis=1, tiled=True)  48.7 us
    psum x1, blocking collectives, body(): lax.psum((jnp.sum(plane_totals, axis=0), jnp.sum(plane_counts, axis=0)),...  39.4 us
  transfers between devices with their start and end apart: 3, of which 3 were waited for; matrix products, arithmetic and copies ran while one was open for 0% of the time, Pallas kernels for 0%

commit v1 on v0

v1 whole, which is shorter than its diff:
```python
import functools
import math

import jax
import jax.numpy as jnp
import ml_dtypes
import numpy as np
from jax import lax
from jax.experimental import pallas as pl
from jax.experimental.pallas import tpu as pltpu
from jax.sharding import PartitionSpec as P

phase_rate = 0.0002
coupling = 0.2
AXES = ("row", "col")
VMEM_LIMIT = 60 * 1024 * 1024


def base_tables(modes):
    grid = 2 * modes
    wave = np.arange(modes) - modes // 2
    turns = np.mod(wave[:, None] * np.arange(grid)[None, :], grid)
    angle = (turns.astype(np.float32) * np.float32(2.0 * math.pi / grid)).astype(np.float64)
    cosine = np.cos(angle).astype(np.float32)
    sine = np.sin(angle).astype(np.float32)
    return cosine, sine


def wide_table(modes):
    cosine, sine = base_tables(modes)
    return np.block([[cosine, sine], [-sine, cosine]]).astype(ml_dtypes.bfloat16)


def shell_counts(modes):
    wave = np.arange(modes, dtype=np.int64) - modes // 2
    squares = wave * wave
    pairs = np.bincount((squares[:, None] + squares[None, :]).ravel())
    total = np.zeros(len(pairs) + int(squares.max()), np.int64)
    for square in squares:
        total[square : square + len(pairs)] += pairs
    shell = np.floor(np.sqrt(np.arange(len(total), dtype=np.float64)) + 0.5).astype(np.int64)
    counts = np.bincount(shell, weights=total, minlength=modes)[:modes]
    return np.maximum(counts, 1.0).astype(np.float32)


def first_kernel(scale, field_ref, tall_ref, out_ref, wide_ref):
    width_x = field_ref.shape[1]
    grid = tall_ref.shape[0] // 2
    lanes = out_ref.shape[2]

    def pair(step, carry):
        x = 2 * step
        rows = []
        for k in range(2):
            rows.append(
                jnp.concatenate([field_ref[0, x + k], field_ref[1, x + k]], axis=1).astype(
                    jnp.bfloat16
                )
            )
        coeffs = jnp.concatenate(rows, axis=0)
        for part in range(2):
            product = (
                lax.dot_general(
                    tall_ref[part * grid : (part + 1) * grid, :],
                    coeffs,
                    (((1,), (1,)), ((), ())),
                    preferred_element_type=jnp.float32,
                )
                * scale
            )
            for k in range(2):
                wide_ref[pl.ds(part * width_x + x + k, grid, stride=2 * width_x), :] = product[
                    :, k * lanes : (k + 1) * lanes
                ]
        return carry

    lax.fori_loop(0, width_x // 2, pair, 0)
    group = out_ref.shape[0] // 16

    def narrow(step, carry):
        start = pl.multiple_of(step * group * width_x, group * width_x)
        block = wide_ref[pl.ds(start, group * width_x), :].astype(jnp.bfloat16)
        out_ref[pl.ds(step * group, group)] = block.reshape(group, width_x, lanes)
        return carry

    lax.fori_loop(0, 16, narrow, 0)


def middle_kernel(rows, cols, scale_in, scale_out, in_ref, wide_ref, tall_ref, out_ref):
    width_x, width_y = in_ref.shape[3], in_ref.shape[4]
    modes = rows * width_x
    grid = 2 * modes
    pieces = []
    for part in range(2):
        for col in range(cols):
            block = jnp.concatenate(
                [in_ref[row * cols + col, 0, part] for row in range(rows)], axis=0
            )
            pieces.append(block)
    lines = jnp.concatenate(pieces, axis=1)
    along_y = (
        jnp.dot(lines, wide_ref[...], preferred_element_type=jnp.float32) * scale_in
    ).astype(jnp.bfloat16)
    stacked = jnp.concatenate([along_y[:, :grid], along_y[:, grid:]], axis=0)
    step = grid // 2
    halves = []
    for start in range(0, grid, step):
        field = (
            jnp.dot(
                tall_ref[...], stacked[:, start : start + step], preferred_element_type=jnp.float32
            )
            * scale_in
        )
        real, imag = field[:grid], field[grid:]
        weight = coupling * (real * real + imag * imag)
        cubic = jnp.concatenate(
            [(weight * real).astype(jnp.bfloat16), (weight * imag).astype(jnp.bfloat16)], axis=0
        )
        halves.append(
            (
                jnp.dot(wide_ref[...], cubic, preferred_element_type=jnp.float32) * scale_out
            ).astype(jnp.bfloat16)
        )
    back = jnp.concatenate(
        [half[:modes] for half in halves] + [half[modes:] for half in halves], axis=1
    )
    back_y = (
        jnp.dot(back, tall_ref[...], preferred_element_type=jnp.float32) * scale_out
    ).astype(jnp.bfloat16)
    for part in range(2):
        for col in range(cols):
            start = part * modes + col * width_y
            for row in range(rows):
                out_ref[row * cols + col, 0, part] = back_y[
                    row * width_x : (row + 1) * width_x, start : start + width_y
                ]


def last_kernel(
    scale,
    nl_ref,
    field_ref,
    tall_ref,
    tri_ref,
    radius_ref,
    cos_xy_ref,
    sin_xy_ref,
    cos_z_ref,
    sin_z_ref,
    out_ref,
    total_ref,
    wide_ref,
):
    width_x, width_y, modes = field_ref.shape[1], field_ref.shape[2], field_ref.shape[3]
    grid = 2 * modes
    half = modes // 2
    group = nl_ref.shape[0] // 16

    def widen(step, carry):
        start = pl.multiple_of(step * group * width_x, group * width_x)
        block = nl_ref[pl.ds(step * group, group)].reshape(group * width_x, width_y)
        wide_ref[pl.ds(start, group * width_x), :] = block.astype(jnp.float32)
        return carry

    lax.fori_loop(0, 16, widen, 0)
    total_ref[...] = jnp.zeros_like(total_ref)
    cos_z, sin_z = cos_z_ref[...], sin_z_ref[...]
    shell_low = lax.broadcasted_iota(jnp.int32, (1, modes), 1).astype(jnp.float32)
    below = jnp.where(shell_low > 0.0, shell_low * shell_low - shell_low, -1.0)
    limits = [below, shell_low * shell_low + shell_low]

    def pair(step, carry):
        x = 2 * step
        columns = []
        for k in range(2):
            columns.append(
                jnp.concatenate(
                    [
                        wide_ref[pl.ds(part * width_x + x + k, grid, stride=2 * width_x), :]
                        for part in range(2)
                    ],
                    axis=0,
                ).astype(jnp.bfloat16)
            )
        lines = jnp.concatenate(columns, axis=1)
        nonlinear = (
            lax.dot_general(
                lines, tall_ref[...], (((0,), (0,)), ((), ())), preferred_element_type=jnp.float32
            )
            * scale
        )
        for k in range(2):
            block = nonlinear[k * width_y : (k + 1) * width_y]
            u = field_ref[0, x + k] - block[:, modes:]
            v = field_ref[1, x + k] + block[:, :modes]
            cos_xy, sin_xy = cos_xy_ref[x + k], sin_xy_ref[x + k]
            cosine = cos_xy * cos_z - sin_xy * sin_z
            sine = sin_xy * cos_z + cos_xy * sin_z
            new_real = u * cosine + v * sine
            new_imag = v * cosine - u * sine
            out_ref[0, x + k] = new_real
            out_ref[1, x + k] = new_imag
            energy = new_real * new_real + new_imag * new_imag
            high = energy.astype(jnp.bfloat16)
            rest = energy - high.astype(jnp.float32)
            middle = rest.astype(jnp.bfloat16)
            low = (rest - middle.astype(jnp.float32)).astype(jnp.bfloat16)
            running = jnp.zeros((width_y, half), jnp.float32)
            for piece in (low, middle, high):
                running += jnp.dot(piece, tri_ref[...], preferred_element_type=jnp.float32)
            radius = radius_ref[x + k]
            parts = []
            for start in range(0, modes, half):
                found = []
                for limit in limits:
                    room = limit[:, start : start + half] - radius
                    index = jnp.floor(jnp.sqrt(jnp.maximum(room, 0.0) + 0.5)).astype(jnp.int32)
                    index = jnp.minimum(index, half - 1)
                    value = jnp.take_along_axis(
                        running, index, axis=1, mode="promise_in_bounds"
                    )
                    found.append(jnp.where(room >= 0.0, value, 0.0))
                parts.append(found[1] - found[0])
            spread = jnp.concatenate(parts, axis=1)
            edge = radius + float(half * half)
            inside = (edge > limits[0]) & (edge <= limits[1])
            spread = spread + jnp.where(inside, energy[:, 0:1], 0.0)
            total_ref[...] += jnp.sum(spread, axis=0, keepdims=True)
        return carry

    lax.fori_loop(0, width_x // 2, pair, 0)


def whole(ndim):
    return pl.BlockSpec(memory_space=pltpu.VMEM)


def geometry(spectral_field):
    width_x, width_y, modes = spectral_field.shape[1:]
    half = modes // 2
    wave_x = lax.axis_index("row") * width_x + jnp.arange(width_x, dtype=jnp.int32) - half
    wave_y = lax.axis_index("col") * width_y + jnp.arange(width_y, dtype=jnp.int32) - half
    wave_z = jnp.arange(modes, dtype=jnp.int32) - half
    return wave_x * wave_x, wave_y * wave_y, wave_z * wave_z


def kernels_body(spectral_field):
    width_x, width_y, modes = spectral_field.shape[1:]
    rows, cols = lax.axis_size("row"), lax.axis_size("col")
    devices = rows * cols
    grid = 2 * modes
    planes = grid // devices
    half = modes // 2
    scale_in = 1.0 / math.sqrt(modes)
    scale_out = math.sqrt(modes) / grid
    table = wide_table(modes)
    wide = jnp.asarray(table)
    tall = jnp.asarray(np.ascontiguousarray(table.T))
    params = pltpu.CompilerParams(vmem_limit_bytes=VMEM_LIMIT)
    along_z = pl.pallas_call(
        functools.partial(first_kernel, scale_in),
        out_shape=jax.ShapeDtypeStruct((2 * grid, width_x, width_y), jnp.bfloat16),
        in_specs=[whole(4), whole(2)],
        out_specs=whole(3),
        scratch_shapes=[pltpu.VMEM((2 * grid * width_x, width_y), jnp.float32)],
        compiler_params=params,
        name="first",
    )(spectral_field, tall)
    along_z = along_z.reshape(devices, planes, 2, width_x, width_y)
    lines = lax.all_to_all(along_z, AXES, split_axis=0, concat_axis=0, tiled=True)
    block = pl.BlockSpec((devices, 1, 2, width_x, width_y), lambda z: (0, z, 0, 0, 0))
    back_y = pl.pallas_call(
        functools.partial(middle_kernel, rows, cols, scale_in, scale_out),
        grid=(planes,),
        out_shape=jax.ShapeDtypeStruct(lines.shape, jnp.bfloat16),
        in_specs=[
            block,
            pl.BlockSpec((grid, 2 * grid), lambda z: (0, 0)),
            pl.BlockSpec((2 * grid, grid), lambda z: (0, 0)),
        ],
        out_specs=block,
        compiler_params=params,
        name="middle",
    )(lines, wide, tall)
    home = lax.all_to_all(back_y, AXES, split_axis=0, concat_axis=0, tiled=True)
    home = home.reshape(2 * grid, width_x, width_y)
    square_x, square_y, square_z = geometry(spectral_field)
    radius = (square_x[:, None] + square_y[None, :]).astype(jnp.float32)[:, :, None]
    angle_xy = phase_rate * radius
    angle_z = phase_rate * square_z.astype(jnp.float32)[None, :]
    distance = np.abs(np.arange(modes) - half)
    triangle = (distance[:, None] <= np.arange(half)[None, :]).astype(ml_dtypes.bfloat16)
    updated_field, totals = pl.pallas_call(
        functools.partial(last_kernel, scale_out),
        out_shape=(
            jax.ShapeDtypeStruct(spectral_field.shape, jnp.float32),
            jax.ShapeDtypeStruct((1, modes), jnp.float32),
        ),
        in_specs=[whole(0)] * 9,
        out_specs=(whole(0), whole(0)),
        scratch_shapes=[pltpu.VMEM((2 * grid * width_x, width_y), jnp.float32)],
        compiler_params=params,
        name="last",
    )(
        home,
        spectral_field,
        tall,
        jnp.asarray(triangle),
        radius,
        jnp.cos(angle_xy),
        jnp.sin(angle_xy),
        jnp.cos(angle_z),
        jnp.sin(angle_z),
    )
    totals = lax.psum(totals[0], AXES)
    return updated_field, totals / jnp.asarray(shell_counts(modes))


def plain_body(spectral_field):
    width_x, width_y, modes = spectral_field.shape[1:]
    rows, cols = lax.axis_size("row"), lax.axis_size("col")
    devices = rows * cols
    grid = 2 * modes
    planes = grid // devices
    scale_in = 1.0 / math.sqrt(modes)
    scale_out = math.sqrt(modes) / grid
    table = jnp.asarray(wide_table(modes)).reshape(2, modes, 2, grid)

    def product(form, first, second, factor):
        out = jnp.einsum(form, first, second, preferred_element_type=jnp.float32)
        return out * factor

    coeffs = spectral_field.astype(jnp.bfloat16)
    along_z = product("pxyj,pjqn->nqxy", coeffs, table, scale_in).astype(jnp.bfloat16)
    lines = lax.all_to_all(along_z, AXES, split_axis=0, concat_axis=0, tiled=True)
    lines = lines.reshape(rows, cols, planes, 2, width_x, width_y)
    lines = lines.transpose(2, 3, 0, 4, 1, 5).reshape(planes, 2, modes, modes)
    along_y = product("zpxy,pyqn->zqxn", lines, table, scale_in).astype(jnp.bfloat16)
    field = product("zpxn,pxqm->zqmn", along_y, table, scale_in)
    real, imag = field[:, 0:1], field[:, 1:2]
    cubic = (coupling * (real * real + imag * imag) * field).astype(jnp.bfloat16)
    back_x = product("zqmn,pxqm->zpxn", cubic, table, scale_out).astype(jnp.bfloat16)
    back_y = product("zqxn,pyqn->zpxy", back_x, table, scale_out).astype(jnp.bfloat16)
    back_y = back_y.reshape(planes, 2, rows, width_x, cols, width_y)
    back_y = back_y.transpose(2, 4, 0, 1, 3, 5).reshape(grid, 2, width_x, width_y)
    home = lax.all_to_all(back_y, AXES, split_axis=0, concat_axis=0, tiled=True)
    nonlinear = product("nqxy,pjqn->pxyj", home, table, scale_out)
    square_x, square_y, square_z = geometry(spectral_field)
    squared = square_x[:, None, None] + square_y[None, :, None] + square_z[None, None, :]
    angle = phase_rate * squared.astype(jnp.float32)
    cosine, sine = jnp.cos(angle), jnp.sin(angle)
    u = spectral_field[0] - nonlinear[1]
    v = spectral_field[1] + nonlinear[0]
    new_real = u * cosine + v * sine
    new_imag = v * cosine - u * sine
    energy = new_real * new_real + new_imag * new_imag
    shell = jnp.floor(jnp.sqrt(squared.astype(jnp.float32)) + 0.5).astype(jnp.int32)
    bins = jnp.arange(modes, dtype=jnp.int32)

    def per_plane(plane):
        one_hot = (plane[1].reshape(-1)[:, None] == bins[None, :]).astype(jnp.float32)
        return jnp.dot(plane[0].reshape(-1), one_hot, precision=lax.Precision.HIGHEST)

    totals = lax.psum(jnp.sum(lax.map(per_plane, (energy, shell)), axis=0), AXES)
    return jnp.stack([new_real, new_imag]), totals / jnp.asarray(shell_counts(modes))


def body(spectral_field):
    width_x, width_y, modes = spectral_field.shape[1:]
    fits = width_x % 16 == 0 and width_y % 128 == 0 and (modes // 2) == 128
    return (kernels_body if fits else plain_body)(spectral_field)


def solution(mesh):
    in_specs = (P(None, "row", "col", None),)
    out_specs = (P(None, "row", "col", None), P())
    return jax.shard_map(body, mesh=mesh, in_specs=in_specs, out_specs=out_specs, check_vma=False)
```

time: 1380 us -> 314 us (0.23)
  other arithmetic: 335 us -> 7.25 us
  matrix products: 323 us -> 0 us
  local copies, waits for them, and re-layouts: 184 us -> 0.01 us
  waiting for transfers between devices: 248 us -> 86.9 us
  blocking collectives: 258 us -> 140 us
  Pallas kernels: 0 us -> 75 us
  starting transfers between devices: 17.9 us -> 3.72 us
    dot_general x40 -> x0, matrix products: 323 us -> none  [the longest x24 162 us: product(): jnp.einsum(einsum_form, first_arg, second_arg, preferred_element_type=jnp...]
    reduce_sum x18 -> x0, other arithmetic: 229 us -> none  [the longest x16 229 us: per_plane(): return (plane_total, jnp.sum(one_hot, axis=0))]
    all_to_all x3 -> x1, waiting for transfers between devices: 248 us -> 86.9 us  [kernels_body(): home = lax.all_to_all(back_y, AXES, split_axis=0, concat_axis=0, tiled=True)]
    all_to_all x1, blocking collectives: 219 us -> 101 us  [kernels_body(): lax.all_to_all(along_z, AXES, split_axis=0, concat_axis=0, tiled=True)]
    pallas_call x0 -> x3, Pallas kernels: none -> 75 us  [the longest x1 41.8 us: kernels_body(): pl.pallas_call(functools.partial(middle_kernel, rows, cols, scale_in, sca...]
    convert_element_type x10 -> x1, other arithmetic: 54.7 us -> 1.16 us  [kernels_body(): (square_x[:, None] + square_y[None, :]).astype(jnp.float32)[:, :, None]]
    squeeze x8 -> x0, local copies, waits for them, and re-layouts: 42.3 us -> none  [the longest x4 21.4 us: rotate(): values_in[1]]
    convert_element_type x4 -> x0, local copies, waits for them, and re-layouts: 41.9 us -> none  [the longest x1 14.6 us: body(): rotate(cubic_term, fwd_x[0], fwd_x[1], 'abc,cd->abd', scale_out)]
  transfers between devices with their start and end apart: 3 -> 1, of which waited for: 3 -> 1; matrix products, arithmetic and copies ran while one was open for 0% -> 2% of each run, Pallas kernels for 0% -> 0%
where the time goes in v1:
time: 314 us; the launch traced here: 313 us
  blocking collectives  140 us (45%)
  waiting for transfers between devices  86.9 us (28%)
  Pallas kernels  75 us (24%)
  other arithmetic  7.25 us (2%)
  starting transfers between devices  3.72 us (1%)
    all_to_all x1, blocking collectives, kernels_body(): lax.all_to_all(along_z, AXES, split_axis=0, concat_axis=0, tiled=True)  101 us
    all_to_all x1, waiting for transfers between devices, kernels_body(): home = lax.all_to_all(back_y, AXES, split_axis=0, concat_axis=0, tiled=True)  86.9 us
    pallas_call x1, Pallas kernels, kernels_body(): pl.pallas_call(functools.partial(middle_kernel, rows, cols, scale_in, sca...  41.8 us
    psum x1, blocking collectives, kernels_body(): totals = lax.psum(totals[0], AXES)  38.8 us
    pallas_call x1, Pallas kernels, kernels_body(): pl.pallas_call(functools.partial(last_kernel, scale_out), out_shape=(jax....  20.5 us
    pallas_call x1, Pallas kernels, kernels_body(): pl.pallas_call(functools.partial(first_kernel, scale_in), out_shape=jax.S...  12.6 us
  transfers between devices with their start and end apart: 1, of which 1 were waited for; matrix products, arithmetic and copies ran while one was open for 2% of the time, Pallas kernels for 0%

profile of v1, /device:TPU:0, one launch (start us, length us, event | category | flops | bytes accessed | tf_op | source)
XLA Modules:
  0.0 313.4 jit_solution(16118027895238786070)
XLA Ops:
  0.6 12.6 %first.1 = bf16[1024,16,128]{2,1,0:T(8,128)(2,1)} custom-call(f32[2,16,128,256]{3,2,1,0:T(8,128)} %field_ref.3, bf16[1024,512]{1,0:T(8,128)(2,1)} %constant.31.clone.tall_ref), custom_call_target="tpu_custom_call" | custom-call | tf_op jit(solution)/shard_map/first/pallas_call | solution.py:260
  13.3 101.1 %all_to_all.10.in_ref = bf16[32,16,2,16,128]{4,3,2,1,0:T(8,128)(2,1)} all-to-all(bf16[32,16,2,16,128]{4,3,2,1,0:T(8,128)(2,1)} %bitcast.3), channel_id=1, replica_groups=mesh['row'=16,'col'=2] {'row','col'}, dimensions={0} | all-to-all | bytes 8388608 | tf_op jit(solution)/shard_map/all_to_all | solution.py:270
  114.3 41.8 %middle.1 = bf16[32,16,2,16,128]{4,3,2,1,0:T(8,128)(2,1)} custom-call(bf16[32,16,2,16,128]{4,3,2,1,0:T(8,128)(2,1)} %all_to_all.10.in_ref, bf16[512,1024]{1,0:T(8,128)(2,1)} %constant.30.clone.wide_ref, bf16[1024,512]{1,0:T(8,128)(2,1)} %constant.31.clone.tall_ref), custom_call_target="tpu_custom_call" | custom-call | tf_op jit(solution)/shard_map/middle/pallas_call | solution.py:272
  156.2 3.7 %all-to-all-start.1 = ((bf16[32,16,2,16,128]{4,3,2,1,0:T(8,128)(2,1)}), bf16[32,16,2,16,128]{4,3,2,1,0:T(8,128)(2,1)}, u32[]{:S(2)}, u32[]{:S(2)}) async-start(bf16[32,16,2,16,128]{4,3,2,1,0:T(8,128)(2,1)} %middle.1), calls=%async_computation.1 | async-start | bytes 8388608 | tf_op jit(solution)/shard_map/all_to_all | solution.py:285
  159.9 0.6 fusion
  160.6 1.2 add_convert_fusion.radius_ref
  161.7 4.9 %multiply_sine_fusion = (f32[16,128,1]{2,1,0:T(8,128)}, f32[16,128,1]{2,1,0:T(8,128)}) fusion(s32[16]{0:T(128)S(1)} %add_multiply_fusion.1, s32[128]{0:T(128)S(1)} %add_multiply_fusion), kind=kLoop, calls=%fused_computation.1 | loop fusion | flops 6144 | bytes 16960 | tf_op jit(solution)/shard_map/sin | solution.py:311
  166.6 86.9 %all-to-all-done.1 = bf16[32,16,2,16,128]{4,3,2,1,0:T(8,128)(2,1)} async-done(((bf16[32,16,2,16,128]{4,3,2,1,0:T(8,128)(2,1)}), bf16[32,16,2,16,128]{4,3,2,1,0:T(8,128)(2,1)}, u32[]{:S(2)}, u32[]{:S(2)}) %all-to-all-start.1) | async-done | bytes 4194336 | tf_op jit(solution)/shard_map/all_to_all | solution.py:285
  253.5 0.0 copy-start
  253.5 20.5 %last.1 = (f32[2,16,128,256]{3,2,1,0:T(8,128)}, f32[1,256]{1,0:T(1,128)}) custom-call(bf16[1024,16,128]{2,1,0:T(8,128)(2,1)} %bitcast.1.nl_ref, f32[2,16,128,256]{3,2,1,0:T(8,128)} %field_ref.3, bf16[1024,512]{1,0:T(8,128)(2,1)} %constant.31.clone.tall_ref, bf16[256,128]{1,0:T(8,128)(2,1)} %constant.32.clone.tri_ref, ...), custom_call_target="tpu_custom_call" | custom-call | tf_op jit(solution)/shard_map/last/pallas_call | solution.py:293
  274.0 38.8 %psum.7 = f32[256]{0:T(256)S(1)} all-reduce(f32[256]{0:T(256)} %bitcast.4), channel_id=1, replica_groups=mesh['row'=16,'col'=2] {'row','col'}, use_global_device_ids=true, to_apply=%region_0.0 | all-reduce | flops 256 | bytes 2048 | tf_op jit(solution)/shard_map/psum | solution.py:315
  312.8 0.0 copy-done
  312.8 0.6 multiply
  (2 shorter events, 0.0 us)
Async XLA Ops:
  156.2 97.4 %all-to-all-start.1 = ((bf16[32,16,2,16,128]{4,3,2,1,0:T(8,128)(2,1)}), bf16[32,16,2,16,128]{4,3,2,1,0:T(8,128)(2,1)}, u32[]{:S(2)}, u32[]{:S(2)}) async-start(bf16[32,16,2,16,128]{4,3,2,1,0:T(8,128)(2,1)} %middle.1), calls=%async_computation.1 | async-start | bytes 8388608 | tf_op jit(solution)/shard_map/all_to_all | solution.py:285
  253.5 59.3 %copy-start = (f32[256]{0:T(256)S(1)}, f32[256]{0:T(256)}, u32[]{:S(2)}) copy-start(f32[256]{0:T(256)} %constant.34) | copy-start | bytes 3076
